TPU v7x, 32 devices: a whole 2x2x4 slice. The times are simulated.
32 devices in a mesh: groups: 2 (over x), blk: 8 (over z, y), rep: 2 (over core).
Axes of the slice: x: 2, y: 2, z: 4, core: 2. Of those that a mesh axis runs over, the one named last changes fastest.
Arguments:
- tokens: bfloat16 [2048, 7168], P(('groups', 'blk', 'rep')), parts along dimension 0, may hold values from -6 to 6
- router_scores: float32 [2048, 8], P(('groups', 'blk', 'rep')), parts along dimension 0, may hold values from -6 to 6
- expert_ids: int32 [2048, 8], P(('groups', 'blk', 'rep')), parts along dimension 0, may hold values from 0 to 255, as said below
- gate_weight: bfloat16 [7168, 4096], P(None, ('blk', 'rep')), may hold values from -0.0625 to 0.0625
- up_weight: bfloat16 [7168, 4096], P(None, ('blk', 'rep')), may hold values from -0.0625 to 0.0625
- down_weight: bfloat16 [4096, 7168], P(('blk', 'rep')), may hold values from -0.125 to 0.125
Outputs:
- moe_out: bfloat16 [2048, 7168], P(('groups', 'blk', 'rep')), parts along dimension 0
There are 2 independent parts, one for each index of `groups`. A program takes and returns all parts, laid end to end along the dimension named above; an argument that names none is the same for every part. Nothing has to cross between parts.
Inputs may be any that keep to these rules, and one draw needn't show every extreme that they name: `expert_ids`: each row names 8 different experts. In the rows of one device (aligned blocks of 64 rows) each expert below 2 is named by at most 2 rows, and in every draw one such expert is named by exactly 2 rows in every block.
All inputs are finite; a program needn't handle non-finite values.
Results may differ from a plain program's by a relative error of at most 0.0068.
Values may be sent and summed in bfloat16 or wider, within the bound.
No kernel may reach another device: no remote copies, remote signals or barrier semaphores. Data moves between devices by JAX's collectives and lax.ppermute only.
A program may use at most 128 MiB of HBM per device.

v0:
```python
import jax
import jax.numpy as jnp
from jax import lax
from jax.sharding import PartitionSpec as P

FF = 2048
CAP = 2


route_scale = 2.5


def project(row_data, w_gate, w_up, w_down):
    gate_proj = jnp.dot(row_data, w_gate, preferred_element_type=jnp.float32)
    up_proj = jnp.dot(row_data, w_up, preferred_element_type=jnp.float32)
    hidden = (jax.nn.silu(gate_proj) * up_proj).astype(jnp.bfloat16)
    return jnp.dot(hidden, w_down, preferred_element_type=jnp.float32)


def expert_rows(row_data, w_gate, w_up, w_down):
    return project(row_data, w_gate, w_up, w_down)


def shards(tokens, router_scores, expert_ids, gate_weight, up_weight, down_weight):
    blk_count = lax.axis_size("blk")
    rep_count = lax.axis_size("rep")
    model_width = tokens.shape[1]
    slice_units = gate_weight.shape[1]
    window_size = blk_count * rep_count * slice_units // FF
    group_size = blk_count // window_size
    sigmoid_scores = jax.nn.sigmoid(router_scores)
    gate_values = route_scale * sigmoid_scores / jnp.sum(sigmoid_scores, axis=1, keepdims=True)
    expert_range = jnp.arange(window_size, dtype=jnp.int32)
    member = expert_ids[:, :, None] == expert_range[None, None, :]
    is_hit = jnp.any(member, axis=1)
    token_weight = jnp.sum(jnp.where(member, gate_values[:, :, None], jnp.float32(0.0)), axis=1)
    slot_rank = jnp.cumsum(is_hit.astype(jnp.int32), axis=0) - 1
    slot_range = jnp.arange(CAP, dtype=jnp.int32)
    placed = (slot_rank.T[:, None, :] == slot_range[None, :, None]) & is_hit.T[:, None, :]
    packed = jnp.einsum(
        "ect,td->ecd", placed.astype(jnp.bfloat16), tokens, preferred_element_type=jnp.float32
    ).astype(jnp.bfloat16)
    counts = jnp.sum(is_hit.astype(jnp.int32), axis=0)
    outgoing = jnp.repeat(packed, group_size, axis=0)
    out_counts = jnp.repeat(counts, group_size)[:, None]
    arrived, arrived_counts = (
        lax.all_to_all(outgoing, "blk", split_axis=0, concat_axis=0, tiled=True),
        lax.all_to_all(out_counts, "blk", split_axis=0, concat_axis=0, tiled=True),
    )
    all_rows, all_counts = (
        lax.all_gather(arrived, "rep", axis=0, tiled=True),
        lax.all_gather(arrived_counts, "rep", axis=0, tiled=True),
    )
    partial_value = expert_rows(
        all_rows.reshape(-1, model_width), gate_weight, up_weight, down_weight
    )
    own_partial = lax.psum_scatter(
        partial_value.reshape(rep_count * blk_count, CAP, model_width),
        "rep",
        scatter_dimension=0,
        tiled=True,
    )
    returned = lax.all_to_all(own_partial, "blk", split_axis=0, concat_axis=0, tiled=True)
    per_expert = jnp.sum(returned.reshape(window_size, group_size, CAP, model_width), axis=1)
    weighted = jnp.where(placed, token_weight.T[:, None, :], jnp.float32(0.0))
    combined = jnp.einsum("ect,ecd->td", weighted, per_expert, precision=lax.Precision.HIGHEST)
    return combined.astype(jnp.bfloat16)


def solution(mesh):
    placed = (
        P(("groups", "blk", "rep"), None),
        P(("groups", "blk", "rep"), None),
        P(("groups", "blk", "rep"), None),
        P(None, ("blk", "rep")),
        P(None, ("blk", "rep")),
        P(("blk", "rep"), None),
    )
    return jax.shard_map(
        shards,
        mesh=mesh,
        in_specs=placed,
        out_specs=P(("groups", "blk", "rep"), None),
        check_vma=False,
    )
```

profile of v0, /device:TPU:0, one launch (start us, length us, event | category | flops | bytes accessed | tf_op | source)
XLA Modules:
  0.0 84.3 jit_solution(1515167165830510171)
XLA Ops:
  6.5 0.8 fusion.11
  7.3 0.1 copy.18
  7.4 0.1 reduce_window_sum.11
  7.5 0.1 copy.19
  7.6 0.1 copy-done
  7.7 0.2 convolution_convert_fusion
  8.0 0.1 broadcast_in_dim.39
  8.1 15.5 %all_to_all.10 = bf16[8,2,7168]{2,1,0:T(2,128)(2,1)S(1)} all-to-all(bf16[8,2,7168]{2,1,0:T(2,128)(2,1)S(1)} %bitcast.20), channel_id=1, replica_groups=mesh['groups'=2,'blk'=8,'rep'=2] {'blk'}, dimensions={0} | all-to-all | bytes 458752 | tf_op jit(solution)/shard_map/all_to_all | solution.py:47
  23.6 2.1 %all_gather.3 = bf16[16,2,7168]{2,1,0:T(2,128)(2,1)S(1)} all-gather(bf16[8,2,7168]{2,1,0:T(2,128)(2,1)S(1)} %all_to_all.10), channel_id=1, replica_groups=mesh['groups'=2,'blk'=8,'rep'=2] {'rep'}, dimensions={0}, use_global_device_ids=true | all-gather | bytes 688128 | tf_op jit(solution)/shard_map/all_gather | solution.py:51
  25.8 0.2 reshape.19
  25.9 2.8 %fusion.19 = f32[32,256]{1,0:T(8,128)S(1)} fusion(bf16[32,7168]{1,0:T(8,128)(2,1)S(1)} %reshape.19, bf16[7168,256]{1,0:T(8,128)(2,1)} %param.9), kind=kOutput, calls=%fused_computation.30 | convolution fusion | flops 117440512 | bytes 4161536 | tf_op jit(solution)/shard_map/dot_general | solution.py:14
  28.7 0.0 copy-start.3
  28.7 5.2 %fusion.2 = f32[32,7168]{1,0:T(8,128)S(1)} fusion(bf16[256,7168]{1,0:T(8,128)(2,1)} %param.11, bf16[32,7168]{1,0:T(8,128)(2,1)S(1)} %reshape.19, bf16[7168,256]{1,0:T(8,128)(2,1)} %param.10, f32[32,256]{1,0:T(8,128)S(1)} %fusion.19), kind=kOutput, calls=%fused_computation.5 | convolution fusion | flops 234930176 | bytes 8749056 | tf_op jit(solution)/shard_map/dot_general | solution.py:17
  34.0 0.0 copy-start.2
  34.0 1.5 %reshape.20 = f32[16,2,7168]{2,1,0:T(2,128)} reshape(f32[32,7168]{1,0:T(8,128)S(1)} %fusion.2) | data formatting | bytes 1835008 | tf_op jit(solution)/shard_map/reshape | solution.py:58
  35.5 0.0 all-reduce.3.cloned.1.call-update
  35.5 0.0 copy-done.3
  35.5 0.6 dynamic-slice
  36.7 16.9 %all-reduce.3.cloned.1.call-done = f32[16,2,7168]{2,1,0:T(2,128)} async-done(((f32[16,2,7168]{2,1,0:T(2,128)}), f32[16,2,7168]{2,1,0:T(2,128)}) %all-reduce.3.cloned.1.call-update) | async-done | bytes 917520
  53.6 1.8 %constant_dynamic-slice_fusion = f32[8,2,7168]{2,1,0:T(2,128)} fusion(f32[16,2,7168]{2,1,0:T(2,128)} %all-reduce.3.cloned.1.call-done, u32[]{:T(128)S(6)} %multiply.1), kind=kLoop, calls=%fused_computation.27 | loop fusion | bytes 917508
  55.4 5.8 %all-to-all-start.1 = ((f32[8,2,7168]{2,1,0:T(2,128)}), f32[8,2,7168]{2,1,0:T(2,128)S(1)}, u32[]{:S(2)}, u32[]{:S(2)}) async-start(f32[8,2,7168]{2,1,0:T(2,128)} %constant_dynamic-slice_fusion), calls=%async_computation.1 | async-start | bytes 917504 | tf_op jit(solution)/shard_map/all_to_all | solution.py:63
  61.3 13.4 %all-to-all-done.1 = f32[8,2,7168]{2,1,0:T(2,128)S(1)} async-done(((f32[8,2,7168]{2,1,0:T(2,128)}), f32[8,2,7168]{2,1,0:T(2,128)S(1)}, u32[]{:S(2)}, u32[]{:S(2)}) %all-to-all-start.1) | async-done | bytes 458784 | tf_op jit(solution)/shard_map/all_to_all | solution.py:63
  74.7 0.1 bitcast_reduce_fusion
  74.9 2.6 %fusion = bf16[64,7168]{1,0:T(8,128)(2,1)} fusion(f32[2,2,7168]{2,1,0:T(2,128)S(1)} %bitcast_reduce_fusion, pred[2,2,64]{2,0,1:T(4,128)(4,1)S(1)} %compare_and_fusion, f32[2,64]{1,0:T(2,128)S(1)} %bitcast.21), kind=kOutput, calls=%fused_computation.1 | convolution fusion | flops 22479104 | bytes 1032960 | tf_op jit(solution)/shard_map/ect,ecd->td/dot_general | solution.py:66
  (11 shorter events, 0.1 us)
Async XLA Ops:
  6.5 1.2 %copy-start = (bf16[64,7168]{1,0:T(8,128)(2,1)S(1)}, bf16[64,7168]{1,0:T(8,128)(2,1)}, u32[]{:S(2)}) copy-start(bf16[64,7168]{1,0:T(8,128)(2,1)} %param.6) | copy-start | bytes 2752516
  6.5 47.1 %all-reduce.3.cloned.1.call-start = ((), (), s32[]{:S(2)}) async-start(), calls=%async_computation.2 | async-start | bytes 1835008
  28.7 6.8 %copy-start.3 = (u32[32]{0:T(128)S(1)}, u32[32]{0:T(128)}, u32[]{:S(2)}) copy-start(u32[32]{0:T(128)} %constant.19) | copy-start | bytes 388
  34.0 27.2 %copy-start.1 = (f32[64,8]{0,1:T(8,128)S(1)}, f32[64,8]{0,1:T(8,128)}, u32[]{:S(2)}) copy-start(f32[64,8]{0,1:T(8,128)} %param.7) | copy-start | bytes 6148
  34.0 27.3 %copy-start.2 = (s32[64,8]{0,1:T(8,128)S(1)}, s32[64,8]{0,1:T(8,128)}, u32[]{:S(2)}) copy-start(s32[64,8]{0,1:T(8,128)} %param.8) | copy-start | bytes 6148
  55.4 19.3 %all-to-all-start.1 = ((f32[8,2,7168]{2,1,0:T(2,128)}), f32[8,2,7168]{2,1,0:T(2,128)S(1)}, u32[]{:S(2)}, u32[]{:S(2)}) async-start(f32[8,2,7168]{2,1,0:T(2,128)} %constant_dynamic-slice_fusion), calls=%async_computation.1 | async-start | bytes 917504 | tf_op jit(solution)/shard_map/all_to_all | solution.py:63
Sparse Core Ops, SparseCore 0:
  35.6 17.9 all-reduce.2
where the time goes:
time: 84.7 us; the launch traced here: 84.3 us
  waiting for transfers between devices  30.3 us (36%)
  blocking collectives  17.7 us (21%)
  between operations  14.1 us (17%)
  matrix products  10.9 us (13%)
  starting transfers between devices  5.81 us (7%)
  local copies, waits for them, and re-layouts  4.5 us (5%)
  other arithmetic  1.09 us (1%)
    unnamed x2, waiting for transfers between devices  16.9 us
    all_to_all x1, blocking collectives, shards(): lax.all_to_all(outgoing, 'blk', split_axis=0, concat_axis=0, tiled=True)  15.5 us
    all_to_all x1, waiting for transfers between devices, shards(): lax.all_to_all(own_partial, 'blk', split_axis=0, concat_axis=0, tiled=True)  13.4 us
    all_to_all x1, starting transfers between devices, shards(): lax.all_to_all(own_partial, 'blk', split_axis=0, concat_axis=0, tiled=True)  5.81 us
    dot_general x1, matrix products, project(): return jnp.dot(hidden, w_down, preferred_element_type=jnp.float32)  5.25 us
    dot_general x1, matrix products, project(): gate_proj = jnp.dot(row_data, w_gate, preferred_element_type=jnp.float32)  2.77 us
    dot_general x1, matrix products, shards(): jnp.einsum('ect,ecd->td', weighted, per_expert, precision=lax.Precision.H...  2.6 us
    unnamed x10, local copies, waits for them, and re-layouts  2.57 us
  transfers between devices with their start and end apart: 2, of which 2 were waited for; matrix products, arithmetic and copies ran while one was open for 1% of the time, Pallas kernels for 0%

commit v1 on v0

v1 whole, which is shorter than its diff:
```python
import jax
import jax.numpy as jnp
from jax import lax
from jax.experimental import pallas as pl
from jax.experimental.pallas import tpu as pltpu
from jax.sharding import PartitionSpec as P

FF = 2048
CAP = 2


route_scale = 2.5


def ffn_kernel(mine_ref, other_ref, gate_ref, up_ref, down_ref, keep_ref, send_ref):
    half = mine_ref.shape[0]
    rows = jnp.concatenate([mine_ref[...], other_ref[...]], axis=0)
    gate_proj = jnp.dot(rows, gate_ref[...], preferred_element_type=jnp.float32)
    up_proj = jnp.dot(rows, up_ref[...], preferred_element_type=jnp.float32)
    hidden = (gate_proj / (1.0 + jnp.exp(-gate_proj)) * up_proj).astype(jnp.bfloat16)
    out = jnp.dot(hidden, down_ref[...], preferred_element_type=jnp.float32)
    keep_ref[...] = out[:half]
    send_ref[...] = out[half:].astype(jnp.bfloat16)


def expert_rows(mine, other, w_gate, w_up, w_down):
    rows, width = mine.shape
    return pl.pallas_call(
        ffn_kernel,
        out_shape=(
            jax.ShapeDtypeStruct((rows, width), jnp.float32),
            jax.ShapeDtypeStruct((rows, width), jnp.bfloat16),
        ),
        in_specs=[pl.BlockSpec(memory_space=pltpu.VMEM)] * 5,
        out_specs=[pl.BlockSpec(memory_space=pltpu.VMEM)] * 2,
        compiler_params=pltpu.CompilerParams(vmem_limit_bytes=40 * 1024 * 1024),
    )(mine, other, w_gate, w_up, w_down)


def shards(tokens, router_scores, expert_ids, gate_weight, up_weight, down_weight):
    blk_count = lax.axis_size("blk")
    rep_count = lax.axis_size("rep")
    model_width = tokens.shape[1]
    slice_units = gate_weight.shape[1]
    window_size = blk_count * rep_count * slice_units // FF
    group_size = blk_count // window_size
    swap = [(0, 1), (1, 0)]
    sigmoid_scores = jax.nn.sigmoid(router_scores)
    gate_values = route_scale * sigmoid_scores / jnp.sum(sigmoid_scores, axis=1, keepdims=True)
    expert_range = jnp.arange(window_size, dtype=jnp.int32)
    member = expert_ids[:, :, None] == expert_range[None, None, :]
    is_hit = jnp.any(member, axis=1)
    token_weight = jnp.sum(jnp.where(member, gate_values[:, :, None], jnp.float32(0.0)), axis=1)
    slot_rank = jnp.cumsum(is_hit.astype(jnp.int32), axis=0) - 1
    slot_range = jnp.arange(CAP, dtype=jnp.int32)
    placed = (slot_rank.T[:, None, :] == slot_range[None, :, None]) & is_hit.T[:, None, :]
    packed = jnp.einsum(
        "ect,td->ecd", placed.astype(jnp.bfloat16), tokens, preferred_element_type=jnp.float32
    ).astype(jnp.bfloat16)
    outgoing = jnp.repeat(packed, group_size, axis=0)
    arrived = lax.all_to_all(outgoing, "blk", split_axis=0, concat_axis=0, tiled=True)
    mine = arrived.reshape(-1, model_width)
    other = lax.ppermute(mine, "rep", swap)
    keep, send = expert_rows(mine, other, gate_weight, up_weight, down_weight)
    taken = lax.ppermute(send, "rep", swap)
    own_partial = (keep + taken.astype(jnp.float32)).astype(jnp.bfloat16)
    returned = lax.all_to_all(
        own_partial.reshape(blk_count, CAP, model_width), "blk", split_axis=0, concat_axis=0, tiled=True
    )
    per_expert = jnp.sum(
        returned.reshape(window_size, group_size, CAP, model_width).astype(jnp.float32), axis=1
    )
    weighted = jnp.where(placed, token_weight.T[:, None, :], jnp.float32(0.0))
    combined = jnp.einsum("ect,ecd->td", weighted, per_expert, precision=lax.Precision.HIGHEST)
    return combined.astype(jnp.bfloat16)


def solution(mesh):
    placed = (
        P(("groups", "blk", "rep"), None),
        P(("groups", "blk", "rep"), None),
        P(("groups", "blk", "rep"), None),
        P(None, ("blk", "rep")),
        P(None, ("blk", "rep")),
        P(("blk", "rep"), None),
    )
    return jax.shard_map(
        shards,
        mesh=mesh,
        in_specs=placed,
        out_specs=P(("groups", "blk", "rep"), None),
        check_vma=False,
    )
```

time: 84.7 us -> 44.8 us (0.53)
  waiting for transfers between devices: 30.3 us -> 11.7 us
  between operations: 14.1 us -> 0.07 us
  matrix products: 10.9 us -> 2.84 us
  local copies, waits for them, and re-layouts: 4.5 us -> 7.39 us
  blocking collectives: 17.7 us -> 15.5 us
  starting transfers between devices: 5.81 us -> 3.65 us
  Pallas kernels: 0 us -> 2.07 us
    unnamed x2 -> x0, waiting for transfers between devices: 16.9 us -> none
    dot_general x2 -> x0, matrix products: 8.02 us -> none  [the longest x1 5.25 us: project(): return jnp.dot(hidden, w_down, preferred_element_type=jnp.float32)]
    all_to_all x1, waiting for transfers between devices: 13.4 us -> 8.87 us  [shards(): lax.all_to_all(own_partial.reshape(blk_count, CAP, model_width), 'blk', s...]
    unnamed x10 -> x12, local copies, waits for them, and re-layouts: 2.57 us -> 6.24 us
    ppermute x0 -> x2, waiting for transfers between devices: none -> 2.83 us  [the longest x1 1.48 us: shards(): other = lax.ppermute(mine, 'rep', swap)]
    all_to_all x1, starting transfers between devices: 5.81 us -> 3.4 us  [shards(): lax.all_to_all(own_partial.reshape(blk_count, CAP, model_width), 'blk', s...]
    all_gather x1 -> x0, blocking collectives: 2.12 us -> none  [shards(): lax.all_gather(arrived, 'rep', axis=0, tiled=True)]
    pallas_call x0 -> x1, Pallas kernels: none -> 2.07 us  [expert_rows(): pl.pallas_call(ffn_kernel, out_shape=(jax.ShapeDtypeStruct((rows, width),...]
  transfers between devices with their start and end apart: 2 -> 3, of which waited for: 2 -> 3; matrix products, arithmetic and copies ran while one was open for 1% -> 0% of each run, Pallas kernels for 0% -> 0%
where the time goes in v1:
time: 44.8 us; the launch traced here: 44.5 us
  blocking collectives  15.5 us (35%)
  waiting for transfers between devices  11.7 us (26%)
  local copies, waits for them, and re-layouts  7.39 us (16%)
  starting transfers between devices  3.65 us (8%)
  matrix products  2.84 us (6%)
  Pallas kernels  2.07 us (5%)
  other arithmetic  1.21 us (3%)
    all_to_all x1, blocking collectives, shards(): lax.all_to_all(outgoing, 'blk', split_axis=0, concat_axis=0, tiled=True)  15.5 us
    all_to_all x1, waiting for transfers between devices, shards(): lax.all_to_all(own_partial.reshape(blk_count, CAP, model_width), 'blk', s...  8.87 us
    unnamed x12, local copies, waits for them, and re-layouts  6.24 us
    all_to_all x1, starting transfers between devices, shards(): lax.all_to_all(own_partial.reshape(blk_count, CAP, model_width), 'blk', s...  3.4 us
    dot_general x1, matrix products, shards(): jnp.einsum('ect,ecd->td', weighted, per_expert, precision=lax.Precision.H...  2.6 us
    pallas_call x1, Pallas kernels, expert_rows(): pl.pallas_call(ffn_kernel, out_shape=(jax.ShapeDtypeStruct((rows, width),...  2.07 us
    ppermute x1, waiting for transfers between devices, shards(): other = lax.ppermute(mine, 'rep', swap)  1.48 us
    ppermute x1, waiting for transfers between devices, shards(): taken = lax.ppermute(send, 'rep', swap)  1.35 us
  transfers between devices with their start and end apart: 3, of which 3 were waited for; matrix products, arithmetic and copies ran while one was open for 0% of the time, Pallas kernels for 0%

profile of v1, /device:TPU:0, one launch (start us, length us, event | category | flops | bytes accessed | tf_op | source)
XLA Modules:
  0.0 44.5 jit_solution(12751828496093776069)
XLA Ops:
  0.0 0.8 %fusion.3 = pred[64,2]{0,1:T(4,128)(4,1)S(1)} fusion(s32[64,8]{0,1:T(8,128)} %param.8), kind=kLoop, calls=%fused_computation.10 | loop fusion | flops 1920 | bytes 2176 | tf_op jit(solution)/shard_map/reduce_or | solution.py:52
  0.8 0.1 copy.18
  0.9 0.1 reduce_window_sum.11
  1.0 0.1 copy.19
  1.1 0.1 copy-done
  1.2 0.2 convolution_convert_fusion
  1.4 0.1 broadcast_in_dim.39
  1.6 15.5 %all_to_all.10 = bf16[8,2,7168]{2,1,0:T(2,128)(2,1)S(1)} all-to-all(bf16[8,2,7168]{2,1,0:T(2,128)(2,1)S(1)} %bitcast.15), channel_id=1, replica_groups=mesh['groups'=2,'blk'=8,'rep'=2] {'blk'}, dimensions={0} | all-to-all | bytes 458752 | tf_op jit(solution)/shard_map/all_to_all | solution.py:61
  17.1 0.1 reshape.19.mine_ref
  17.2 0.1 collective-permute-start
  17.3 1.5 %collective-permute-done.other_ref = bf16[16,7168]{1,0:T(8,128)(2,1)S(1)} collective-permute-done((bf16[16,7168]{1,0:T(8,128)(2,1)S(1)}, bf16[16,7168]{1,0:T(8,128)(2,1)S(1)}, u32[]{:S(2)}, u32[]{:S(2)}) %collective-permute-start) | collective-permute-done | bytes 229408 | tf_op jit(solution)/shard_map/ppermute | solution.py:63
  18.8 2.0 %copy-done.1 = bf16[7168,256]{1,0:T(8,128)(2,1)S(1)} copy-done((bf16[7168,256]{1,0:T(8,128)(2,1)S(1)}, bf16[7168,256]{1,0:T(8,128)(2,1)}, u32[]{:S(2)}) %copy-start.1) | copy-done | bytes 3670040
  20.8 2.0 %copy-done.2 = bf16[7168,256]{1,0:T(8,128)(2,1)S(1)} copy-done((bf16[7168,256]{1,0:T(8,128)(2,1)S(1)}, bf16[7168,256]{1,0:T(8,128)(2,1)}, u32[]{:S(2)}) %copy-start.2) | copy-done | bytes 3670040
  22.8 2.0 %copy-done.3 = bf16[256,7168]{1,0:T(8,128)(2,1)S(1)} copy-done((bf16[256,7168]{1,0:T(8,128)(2,1)S(1)}, bf16[256,7168]{1,0:T(8,128)(2,1)}, u32[]{:S(2)}) %copy-start.3) | copy-done | bytes 3670040
  24.9 2.1 %shard_map.64 = (f32[16,7168]{1,0:T(8,128)S(1)}, bf16[16,7168]{1,0:T(8,128)(2,1)S(1)}) custom-call(bf16[16,7168]{1,0:T(8,128)(2,1)S(1)} %reshape.19.mine_ref, bf16[16,7168]{1,0:T(8,128)(2,1)S(1)} %collective-permute-done.other_ref, bf16[7168,256]{1,0:T(8,128)(2,1)S(1)} %copy-done.1, bf16[7168,256]{1,0:T(8,128)(2,1)S(1)} %copy-done.2, ...), custom_call_target="tpu_custom_call" | custom-call | tf_op jit(solution)/shard_map/pallas_call | solution.py:28
  26.9 0.2 collective-permute-start.1
  27.1 1.4 %collective-permute-done.1 = bf16[16,7168]{1,0:T(8,128)(2,1)S(1)} collective-permute-done((bf16[16,7168]{1,0:T(8,128)(2,1)S(1)}, bf16[16,7168]{1,0:T(8,128)(2,1)S(1)}, u32[]{:S(2)}, u32[]{:S(2)}) %collective-permute-start.1) | collective-permute-done | bytes 229408 | tf_op jit(solution)/shard_map/ppermute | solution.py:65
  28.5 0.8 %reshape.20 = bf16[8,2,7168]{2,1,0:T(2,128)(2,1)} reshape(bf16[16,7168]{1,0:T(8,128)(2,1)S(1)} %add_convert_fusion) | data formatting | bytes 458752 | tf_op jit(solution)/shard_map/reshape | solution.py:68
  29.3 3.4 %all-to-all-start.1 = ((bf16[8,2,7168]{2,1,0:T(2,128)(2,1)}), bf16[8,2,7168]{2,1,0:T(2,128)(2,1)S(1)}, u32[]{:S(2)}, u32[]{:S(2)}) async-start(bf16[8,2,7168]{2,1,0:T(2,128)(2,1)} %reshape.20), calls=%async_computation.1 | async-start | bytes 458752 | tf_op jit(solution)/shard_map/all_to_all | solution.py:67
  32.7 0.0 copy-done.4
  32.8 0.0 copy-done.5
  32.8 8.9 %all-to-all-done.1 = bf16[8,2,7168]{2,1,0:T(2,128)(2,1)S(1)} async-done(((bf16[8,2,7168]{2,1,0:T(2,128)(2,1)}), bf16[8,2,7168]{2,1,0:T(2,128)(2,1)S(1)}, u32[]{:S(2)}, u32[]{:S(2)}) %all-to-all-start.1) | async-done | bytes 229408 | tf_op jit(solution)/shard_map/all_to_all | solution.py:67
  41.7 0.2 convert_reduce_fusion
  41.9 2.6 %fusion = bf16[64,7168]{1,0:T(8,128)(2,1)} fusion(f32[2,2,7168]{2,1,0:T(2,128)S(1)} %convert_reduce_fusion, pred[2,2,64]{2,0,1:T(4,128)(4,1)S(1)} %compare_and_fusion, f32[2,64]{1,0:T(2,128)S(1)} %bitcast.16), kind=kOutput, calls=%fused_computation.1 | convolution fusion | flops 22479104 | bytes 1032960 | tf_op jit(solution)/shard_map/ect,ecd->td/dot_general | solution.py:74
  (13 shorter events, 0.1 us)
Async XLA Ops:
  0.0 1.2 %copy-start = (bf16[64,7168]{1,0:T(8,128)(2,1)S(1)}, bf16[64,7168]{1,0:T(8,128)(2,1)}, u32[]{:S(2)}) copy-start(bf16[64,7168]{1,0:T(8,128)(2,1)} %param.6) | copy-start | bytes 2752516
  17.1 15.6 %copy-start.4 = (f32[64,8]{0,1:T(8,128)S(1)}, f32[64,8]{0,1:T(8,128)}, u32[]{:S(2)}) copy-start(f32[64,8]{0,1:T(8,128)} %param.7) | copy-start | bytes 6148
  17.1 15.6 %copy-start.5 = (s32[64,8]{0,1:T(8,128)S(1)}, s32[64,8]{0,1:T(8,128)}, u32[]{:S(2)}) copy-start(s32[64,8]{0,1:T(8,128)} %param.8) | copy-start | bytes 6148
  17.2 1.6 %collective-permute-start = (bf16[16,7168]{1,0:T(8,128)(2,1)S(1)}, bf16[16,7168]{1,0:T(8,128)(2,1)S(1)}, u32[]{:S(2)}, u32[]{:S(2)}) collective-permute-start(bf16[16,7168]{1,0:T(8,128)(2,1)S(1)} %reshape.19.mine_ref), channel_id=1, source_target_pairs={{0,1},{1,0},{2,3},{3,2},{4,5},{5,4},{6,7},{7,6},{8,9},{9,8},{10,11... | collective-permute-start | bytes 688136 | tf_op jit(solution)/shard_map/ppermute | solution.py:63
  18.8 2.0 %copy-start.1 = (bf16[7168,256]{1,0:T(8,128)(2,1)S(1)}, bf16[7168,256]{1,0:T(8,128)(2,1)}, u32[]{:S(2)}) copy-start(bf16[7168,256]{1,0:T(8,128)(2,1)} %gate_ref.1) | copy-start | bytes 11010052
  20.8 2.0 %copy-start.2 = (bf16[7168,256]{1,0:T(8,128)(2,1)S(1)}, bf16[7168,256]{1,0:T(8,128)(2,1)}, u32[]{:S(2)}) copy-start(bf16[7168,256]{1,0:T(8,128)(2,1)} %up_ref.1) | copy-start | bytes 11010052
  22.8 2.0 %copy-start.3 = (bf16[256,7168]{1,0:T(8,128)(2,1)S(1)}, bf16[256,7168]{1,0:T(8,128)(2,1)}, u32[]{:S(2)}) copy-start(bf16[256,7168]{1,0:T(8,128)(2,1)} %down_ref.1) | copy-start | bytes 11010052
  26.9 1.5 %collective-permute-start.1 = (bf16[16,7168]{1,0:T(8,128)(2,1)S(1)}, bf16[16,7168]{1,0:T(8,128)(2,1)S(1)}, u32[]{:S(2)}, u32[]{:S(2)}) collective-permute-start(bf16[16,7168]{1,0:T(8,128)(2,1)S(1)} %get-tuple-element.8), channel_id=1, source_target_pairs={{0,1},{1,0},{2,3},{3,2},{4,5},{5,4},{6,7},{7,6},{8,9},{9,8},{10,11... | collective-permute-start | bytes 688136 | tf_op jit(solution)/shard_map/ppermute | solution.py:65
  29.3 12.4 %all-to-all-start.1 = ((bf16[8,2,7168]{2,1,0:T(2,128)(2,1)}), bf16[8,2,7168]{2,1,0:T(2,128)(2,1)S(1)}, u32[]{:S(2)}, u32[]{:S(2)}) async-start(bf16[8,2,7168]{2,1,0:T(2,128)(2,1)} %reshape.20), calls=%async_computation.1 | async-start | bytes 458752 | tf_op jit(solution)/shard_map/all_to_all | solution.py:67

commit v2 on v1

v2 whole, which is shorter than its diff:
```python
from functools import partial

import jax
import jax.numpy as jnp
from jax import lax
from jax.experimental import pallas as pl
from jax.experimental.pallas import tpu as pltpu
from jax.sharding import PartitionSpec as P

FF = 2048
CAP = 2


route_scale = 2.5
LANES = 128
PREFETCH_COST = 10**9
VMEM = pl.BlockSpec(memory_space=pltpu.VMEM)
HBM = pl.BlockSpec(memory_space=pltpu.HBM)


def slots_of(ids, rows, window_size, group_size):
    top, count = ids.shape
    index = lax.broadcasted_iota(jnp.int32, (rows, count), 0)
    own_expert = lax.axis_index("blk") // group_size
    order = jnp.where(index < window_size * CAP, own_expert ^ (index // CAP), -1)
    members = [ids[slot : slot + 1] == order for slot in range(top)]
    hit = jnp.zeros((rows, count), jnp.float32)
    for member in members:
        hit = jnp.where(member, 1.0, hit)
    from_index = lax.broadcasted_iota(jnp.int32, (count, count), 0)
    to_index = lax.broadcasted_iota(jnp.int32, (count, count), 1)
    upper = jnp.where(from_index <= to_index, 1.0, 0.0).astype(jnp.bfloat16)
    rank = jnp.dot(hit.astype(jnp.bfloat16), upper, preferred_element_type=jnp.float32)
    placed = jnp.where(rank == (index % CAP + 1).astype(jnp.float32), hit, 0.0)
    return members, placed


def pack_kernel(window_size, group_size, ids_ref, tokens_ref, *refs):
    *packet_refs, ids_near, tokens_near, sems = refs
    ids_copy = pltpu.make_async_copy(ids_ref, ids_near, sems.at[0])
    tokens_copy = pltpu.make_async_copy(tokens_ref, tokens_near, sems.at[1])
    ids_copy.start()
    tokens_copy.start()
    rows = -(-window_size * CAP // 16) * 16
    ids_copy.wait()
    _, placed = slots_of(ids_near[...], rows, window_size, group_size)
    tokens_copy.wait()
    packed = jnp.dot(placed.astype(jnp.bfloat16), tokens_near[...], preferred_element_type=jnp.float32)
    for index, ref in enumerate(packet_refs):
        ref[...] = packed[index * CAP : (index + 1) * CAP].astype(jnp.bfloat16)


def weigh_kernel(window_size, group_size, scores_ref, ids_ref, weight_ref):
    sigmoid_scores = 1.0 / (1.0 + jnp.exp(-scores_ref[...]))
    gate_values = route_scale * sigmoid_scores / jnp.sum(sigmoid_scores, axis=0, keepdims=True)
    members, placed = slots_of(ids_ref[...], LANES, window_size, group_size)
    weight = jnp.zeros(placed.shape, jnp.float32)
    for slot, member in enumerate(members):
        weight = jnp.where(member, gate_values[slot : slot + 1], weight)
    weight_ref[...] = (placed * weight).T


def merge_kernel(*refs):
    out_ref = refs[-1]
    pieces = [ref[...].astype(jnp.float32) for ref in refs[:-1]]
    out_ref[...] = jnp.concatenate(pieces, axis=0).astype(jnp.bfloat16)


def merge(pieces, cost=0):
    rows = sum(piece.shape[0] for piece in pieces)
    return pl.pallas_call(
        merge_kernel,
        out_shape=jax.ShapeDtypeStruct((rows, pieces[0].shape[1]), jnp.bfloat16),
        in_specs=[VMEM] * len(pieces),
        out_specs=VMEM,
        cost_estimate=pl.CostEstimate(flops=cost, bytes_accessed=cost, transcendentals=0) if cost else None,
        compiler_params=pltpu.CompilerParams(vmem_limit_bytes=12 * 1024 * 1024),
    )(*pieces)


def fetch_kernel(source_ref, near_ref, sem):
    copy = pltpu.make_async_copy(source_ref, near_ref, sem)
    copy.start()
    copy.wait()


def fetch(array):
    return pl.pallas_call(
        fetch_kernel,
        out_shape=pltpu.VMEM(array.shape, array.dtype),
        in_specs=[HBM],
        out_specs=VMEM,
        scratch_shapes=[pltpu.SemaphoreType.DMA],
        compiler_params=pltpu.CompilerParams(vmem_limit_bytes=1024 * 1024),
    )(array)


def ffn_kernel(mine_ref, other_ref, gate_ref, up_ref, down_ref, keep_ref, send_ref):
    half = mine_ref.shape[0]
    blocks, block_rows, _ = keep_ref.shape
    rows = jnp.concatenate([mine_ref[...], other_ref[...]], axis=0)
    gate_proj = jnp.dot(rows, gate_ref[...], preferred_element_type=jnp.float32)
    up_proj = jnp.dot(rows, up_ref[...], preferred_element_type=jnp.float32)
    hidden = (gate_proj / (1.0 + jnp.exp(-gate_proj)) * up_proj).astype(jnp.bfloat16)
    out = jnp.dot(hidden, down_ref[...], preferred_element_type=jnp.float32)
    for block in range(blocks):
        first = block * block_rows
        keep_ref[block] = out[first : first + block_rows]
        send_ref[block] = out[half + first : half + first + block_rows].astype(jnp.bfloat16)


def expert_rows(mine, other, w_gate, w_up, w_down, blocks):
    rows, width = mine.shape
    shape = (blocks, rows // blocks, width)
    return pl.pallas_call(
        ffn_kernel,
        out_shape=(
            jax.ShapeDtypeStruct(shape, jnp.float32),
            jax.ShapeDtypeStruct(shape, jnp.bfloat16),
        ),
        in_specs=[VMEM] * 5,
        out_specs=(VMEM, VMEM),
        compiler_params=pltpu.CompilerParams(vmem_limit_bytes=28 * 1024 * 1024),
    )(mine, other, w_gate, w_up, w_down)


def combine_kernel(weight_ref, *refs):
    *part_refs, out_ref, stage_ref, sems = refs
    chunks = sems.shape[0]
    step = stage_ref.shape[1] // chunks
    weight = weight_ref[...]
    columns = [weight[:, column : column + 1] for column in range(len(part_refs) * CAP)]
    copies = []
    for chunk in range(chunks):
        span = pl.ds(chunk * step, step)
        total = jnp.zeros((stage_ref.shape[0], step), jnp.float32)
        for index, ref in enumerate(part_refs):
            part = ref[:, span].astype(jnp.float32)
            for slot in range(CAP):
                total = total + columns[index * CAP + slot] * part[slot : slot + 1]
        stage_ref[:, span] = total.astype(jnp.bfloat16)
        copies.append(
            pltpu.make_async_copy(stage_ref.at[:, span], out_ref.at[:, span], sems.at[chunk])
        )
        copies[-1].start()
    for copy in copies:
        copy.wait()


def combine(weight, parts, count):
    width = parts[0].shape[1]
    chunks = 7 if width % (7 * LANES) == 0 else 1
    return pl.pallas_call(
        combine_kernel,
        out_shape=jax.ShapeDtypeStruct((count, width), jnp.bfloat16),
        in_specs=[VMEM] * (len(parts) + 1),
        out_specs=HBM,
        scratch_shapes=[pltpu.VMEM((count, width), jnp.bfloat16), pltpu.SemaphoreType.DMA((chunks,))],
        compiler_params=pltpu.CompilerParams(vmem_limit_bytes=16 * 1024 * 1024),
    )(weight, *parts)


def shards(tokens, router_scores, expert_ids, gate_weight, up_weight, down_weight):
    blk_count = lax.axis_size("blk")
    rep_count = lax.axis_size("rep")
    count, model_width = tokens.shape
    slice_units = gate_weight.shape[1]
    window_size = blk_count * rep_count * slice_units // FF
    group_size = blk_count // window_size
    swap = [(0, 1), (1, 0)]

    def across(value, mask):
        return lax.ppermute(value, "blk", [(s, s ^ mask) for s in range(blk_count)])

    packets = pl.pallas_call(
        partial(pack_kernel, window_size, group_size),
        out_shape=[pltpu.VMEM((CAP, model_width), jnp.bfloat16)] * window_size,
        in_specs=[HBM] * 2,
        out_specs=[VMEM] * window_size,
        scratch_shapes=[
            pltpu.VMEM(expert_ids.shape[::-1], expert_ids.dtype),
            pltpu.VMEM(tokens.shape, tokens.dtype),
            pltpu.SemaphoreType.DMA((2,)),
        ],
        compiler_params=pltpu.CompilerParams(vmem_limit_bytes=66_500_000),
    )(expert_ids.T, tokens)
    far = []
    for k in range(1, window_size):
        far.append(across(packets[k], k * group_size))
    weight = pl.pallas_call(
        partial(weigh_kernel, window_size, group_size),
        out_shape=pltpu.VMEM((count, LANES), jnp.float32),
        in_specs=[VMEM] * 2,
        out_specs=VMEM,
        cost_estimate=pl.CostEstimate(flops=PREFETCH_COST, bytes_accessed=PREFETCH_COST, transcendentals=0),
        compiler_params=pltpu.CompilerParams(vmem_limit_bytes=2 * 1024 * 1024),
    )(router_scores.T, expert_ids.T)
    rows = merge([packets[0]] + far, cost=PREFETCH_COST)
    near = []
    for k in range(1, group_size):
        near.append(across(rows, k))
    down_near = fetch(down_weight)
    mine = merge([rows] + near)
    other = lax.ppermute(mine, "rep", swap)
    keep, send = expert_rows(mine, other, gate_weight, up_weight, down_near, group_size)
    taken = lax.ppermute(send, "rep", swap)
    total = keep + taken.astype(jnp.float32)
    leaving = total.astype(jnp.bfloat16)
    back = [across(leaving[k], k) for k in range(1, group_size)]
    block = total[0]
    for value in back:
        block = block + value.astype(jnp.float32)
    home = block[CAP:].astype(jnp.bfloat16)
    parts = [block] + [
        across(home[(k - 1) * CAP : k * CAP], k * group_size) for k in range(1, window_size)
    ]
    return combine(weight, parts, count)


def solution(mesh):
    placed = (
        P(("groups", "blk", "rep"), None),
        P(("groups", "blk", "rep"), None),
        P(("groups", "blk", "rep"), None),
        P(None, ("blk", "rep")),
        P(None, ("blk", "rep")),
        P(("blk", "rep"), None),
    )
    return jax.shard_map(
        shards,
        mesh=mesh,
        in_specs=placed,
        out_specs=P(("groups", "blk", "rep"), None),
        check_vma=False,
    )
```

time: 44.8 us -> 36.3 us (0.81)
  blocking collectives: 15.5 us -> 0 us
  starting transfers between devices: 3.65 us -> 14.3 us
  local copies, waits for them, and re-layouts: 7.39 us -> 1.71 us
  Pallas kernels: 2.07 us -> 5.67 us
  matrix products: 2.84 us -> 0 us
  waiting for transfers between devices: 11.7 us -> 14.1 us
  other arithmetic: 1.21 us -> 0.22 us
    all_to_all x1 -> x0, blocking collectives: 15.5 us -> none  [shards(): lax.all_to_all(outgoing, 'blk', split_axis=0, concat_axis=0, tiled=True)]
    ppermute x0 -> x8, starting transfers between devices: none -> 14.2 us  [across(): return lax.ppermute(value, 'blk', [(s, s ^ mask) for s in range(blk_count)])]
    ppermute x0 -> x8, waiting for transfers between devices: none -> 11.4 us  [across(): return lax.ppermute(value, 'blk', [(s, s ^ mask) for s in range(blk_count)])]
    all_to_all x1 -> x0, waiting for transfers between devices: 8.87 us -> none  [shards(): lax.all_to_all(own_partial.reshape(blk_count, CAP, model_width), 'blk', s...]
    unnamed x12 -> x10, local copies, waits for them, and re-layouts: 6.24 us -> 1.61 us
    pallas_call x1 -> x7, Pallas kernels: 2.07 us -> 5.67 us  [the longest x1 2.08 us: expert_rows(): pl.pallas_call(ffn_kernel, out_shape=(jax.ShapeDtypeStruct(shape, jnp.flo...]
    all_to_all x1 -> x0, starting transfers between devices: 3.4 us -> none  [shards(): lax.all_to_all(own_partial.reshape(blk_count, CAP, model_width), 'blk', s...]
    dot_general x2 -> x0, matrix products: 2.84 us -> none  [the longest x1 2.6 us: shards(): jnp.einsum('ect,ecd->td', weighted, per_expert, precision=lax.Precision.H...]
  transfers between devices with their start and end apart: 3 -> 10, of which waited for: 3 -> 10; matrix products, arithmetic and copies ran while one was open for 0% -> 0% of each run, Pallas kernels for 0% -> 1%
where the time goes in v2:
time: 36.3 us; the launch traced here: 36.1 us
  starting transfers between devices  14.3 us (39%)
  waiting for transfers between devices  14.1 us (39%)
  Pallas kernels  5.67 us (16%)
  local copies, waits for them, and re-layouts  1.71 us (5%)
    ppermute x8, starting transfers between devices, across(): return lax.ppermute(value, 'blk', [(s, s ^ mask) for s in range(blk_count)])  14.2 us
    ppermute x8, waiting for transfers between devices, across(): return lax.ppermute(value, 'blk', [(s, s ^ mask) for s in range(blk_count)])  11.4 us
    pallas_call x1, Pallas kernels, expert_rows(): pl.pallas_call(ffn_kernel, out_shape=(jax.ShapeDtypeStruct(shape, jnp.flo...  2.08 us
    unnamed x10, local copies, waits for them, and re-layouts  1.61 us
    pallas_call x1, Pallas kernels, combine(): pl.pallas_call(combine_kernel, out_shape=jax.ShapeDtypeStruct((count, wid...  1.58 us
    ppermute x1, waiting for transfers between devices, shards(): taken = lax.ppermute(send, 'rep', swap)  1.48 us
    pallas_call x1, Pallas kernels, shards(): pl.pallas_call(partial(pack_kernel, window_size, group_size), out_shape=[...  1.46 us
    ppermute x1, waiting for transfers between devices, shards(): other = lax.ppermute(mine, 'rep', swap)  1.18 us
  transfers between devices with their start and end apart: 10, of which 10 were waited for; matrix products, arithmetic and copies ran while one was open for 0% of the time, Pallas kernels for 1%

profile of v2, /device:TPU:0, one launch (start us, length us, event | category | flops | bytes accessed | tf_op | source)
XLA Modules:
  0.0 36.1 jit_solution(11300046046845931535)
XLA Ops:
  0.0 1.5 %shard_map.65 = (bf16[2,7168]{1,0:T(2,128)(2,1)S(1)}, bf16[2,7168]{1,0:T(2,128)(2,1)S(1)}) custom-call(s32[8,64]{1,0:T(8,128)} %bitcast.16, bf16[64,7168]{1,0:T(8,128)(2,1)} %tokens_ref.1), custom_call_target="tpu_custom_call" | custom-call | tf_op jit(solution)/shard_map/pallas_call | solution.py:175
  1.5 4.1 %collective-permute-start = (bf16[2,7168]{1,0:T(2,128)(2,1)S(1)}, bf16[2,7168]{1,0:T(2,128)(2,1)S(1)}, u32[]{:S(2)}, u32[]{:S(2)}) collective-permute-start(bf16[2,7168]{1,0:T(2,128)(2,1)S(1)} %get-tuple-element.10), channel_id=1, source_target_pairs={{0,8},{2,10},{4,12},{6,14},{8,0},{10,2},{12,4},{14,6},{1,9},{3,11}... | collective-permute-start | bytes 86024 | tf_op jit(solution)/shard_map/ppermute | solution.py:173
  5.6 1.9 %collective-permute-done.refs_1_ = bf16[2,7168]{1,0:T(2,128)(2,1)S(1)} collective-permute-done((bf16[2,7168]{1,0:T(2,128)(2,1)S(1)}, bf16[2,7168]{1,0:T(2,128)(2,1)S(1)}, u32[]{:S(2)}, u32[]{:S(2)}) %collective-permute-start) | collective-permute-done | bytes 28704 | tf_op jit(solution)/shard_map/ppermute | solution.py:173
  7.5 2.1 %collective-permute-start.1 = (bf16[4,7168]{1,0:T(4,128)(2,1)S(1)}, bf16[4,7168]{1,0:T(4,128)(2,1)S(1)}, u32[]{:S(2)}, u32[]{:S(2)}) collective-permute-start(bf16[4,7168]{1,0:T(4,128)(2,1)S(1)} %shard_map.66.refs_0_), channel_id=1, source_target_pairs={{0,2},{2,0},{4,6},{6,4},{8,10},{10,8},{12,14},{14,12},{1,3},{3,1},... | collective-permute-start | bytes 172040 | tf_op jit(solution)/shard_map/ppermute | solution.py:173
  9.6 1.4 %collective-permute-start.2 = (bf16[4,7168]{1,0:T(4,128)(2,1)S(1)}, bf16[4,7168]{1,0:T(4,128)(2,1)S(1)}, u32[]{:S(2)}, u32[]{:S(2)}) collective-permute-start(bf16[4,7168]{1,0:T(4,128)(2,1)S(1)} %shard_map.66.refs_0_), channel_id=1, source_target_pairs={{0,4},{2,6},{4,0},{6,2},{8,12},{10,14},{12,8},{14,10},{1,5},{3,7},... | collective-permute-start | bytes 172040 | tf_op jit(solution)/shard_map/ppermute | solution.py:173
  11.1 0.8 %collective-permute-done.1.refs_1_ = bf16[4,7168]{1,0:T(4,128)(2,1)S(1)} collective-permute-done((bf16[4,7168]{1,0:T(4,128)(2,1)S(1)}, bf16[4,7168]{1,0:T(4,128)(2,1)S(1)}, u32[]{:S(2)}, u32[]{:S(2)}) %collective-permute-start.1) | collective-permute-done | bytes 57376 | tf_op jit(solution)/shard_map/ppermute | solution.py:173
  12.0 1.8 %collective-permute-done.2.refs_2_ = bf16[4,7168]{1,0:T(4,128)(2,1)S(1)} collective-permute-done((bf16[4,7168]{1,0:T(4,128)(2,1)S(1)}, bf16[4,7168]{1,0:T(4,128)(2,1)S(1)}, u32[]{:S(2)}, u32[]{:S(2)}) %collective-permute-start.2) | collective-permute-done | bytes 57376 | tf_op jit(solution)/shard_map/ppermute | solution.py:173
  13.8 2.3 %collective-permute-done.3.refs_3_ = bf16[4,7168]{1,0:T(4,128)(2,1)S(1)} collective-permute-done((bf16[4,7168]{1,0:T(4,128)(2,1)S(1)}, bf16[4,7168]{1,0:T(4,128)(2,1)S(1)}, u32[]{:S(2)}, u32[]{:S(2)}) %collective-permute-start.3) | collective-permute-done | bytes 57376 | tf_op jit(solution)/shard_map/ppermute | solution.py:173
  16.2 0.3 shard_map.68.down_ref
  16.5 1.2 %collective-permute-done.4.other_ref = bf16[16,7168]{1,0:T(8,128)(2,1)S(1)} collective-permute-done((bf16[16,7168]{1,0:T(8,128)(2,1)S(1)}, bf16[16,7168]{1,0:T(8,128)(2,1)S(1)}, u32[]{:S(2)}, u32[]{:S(2)}) %collective-permute-start.4) | collective-permute-done | bytes 229408 | tf_op jit(solution)/shard_map/ppermute | solution.py:204
  17.7 0.5 %copy-done.1 = bf16[7168,256]{1,0:T(8,128)(2,1)S(1)} copy-done((bf16[7168,256]{1,0:T(8,128)(2,1)S(1)}, bf16[7168,256]{1,0:T(8,128)(2,1)}, u32[]{:S(2)}) %copy-start.1) | copy-done | bytes 3670040
  18.2 1.1 %copy-done.2 = bf16[7168,256]{1,0:T(8,128)(2,1)S(1)} copy-done((bf16[7168,256]{1,0:T(8,128)(2,1)S(1)}, bf16[7168,256]{1,0:T(8,128)(2,1)}, u32[]{:S(2)}) %copy-start.2) | copy-done | bytes 3670040
  19.3 2.1 %shard_map.69 = (f32[4,4,7168]{2,1,0:T(4,128)S(1)}, bf16[4,4,7168]{2,1,0:T(4,128)(2,1)S(1)}) custom-call(bf16[16,7168]{1,0:T(8,128)(2,1)S(1)} %shard_map.67.mine_ref, bf16[16,7168]{1,0:T(8,128)(2,1)S(1)} %collective-permute-done.4.other_ref, bf16[7168,256]{1,0:T(8,128)(2,1)S(1)} %copy-done.1, bf16[7168,256]{1,0:T(8,128)(2,1)S(1)} %copy-done.2, ...), custom_call_target="tpu_custom_call" | custom-call | tf_op jit(solution)/shard_map/pallas_call | solution.py:115
  21.4 1.5 %collective-permute-done.5 = bf16[4,4,7168]{2,1,0:T(4,128)(2,1)S(1)} collective-permute-done((bf16[4,4,7168]{2,1,0:T(4,128)(2,1)S(1)}, bf16[4,4,7168]{2,1,0:T(4,128)(2,1)S(1)}, u32[]{:S(2)}, u32[]{:S(2)}) %collective-permute-start.5) | collective-permute-done | bytes 229408 | tf_op jit(solution)/shard_map/ppermute | solution.py:206
  23.2 0.6 %collective-permute-start.6 = (bf16[4,7168]{1,0:T(4,128)(2,1)S(1)}, bf16[4,7168]{1,0:T(4,128)(2,1)S(1)}, u32[]{:S(2)}, u32[]{:S(2)}) collective-permute-start(bf16[4,7168]{1,0:T(4,128)(2,1)S(1)} %get-tuple-element.15), channel_id=1, source_target_pairs={{0,2},{2,0},{4,6},{6,4},{8,10},{10,8},{12,14},{14,12},{1,3},{3,1},... | collective-permute-start | bytes 172040 | tf_op jit(solution)/shard_map/ppermute | solution.py:173
  23.7 0.7 %collective-permute-start.7 = (bf16[4,7168]{1,0:T(4,128)(2,1)S(1)}, bf16[4,7168]{1,0:T(4,128)(2,1)S(1)}, u32[]{:S(2)}, u32[]{:S(2)}) collective-permute-start(bf16[4,7168]{1,0:T(4,128)(2,1)S(1)} %get-tuple-element.17), channel_id=1, source_target_pairs={{0,4},{2,6},{4,0},{6,2},{8,12},{10,14},{12,8},{14,10},{1,5},{3,7},... | collective-permute-start | bytes 172040 | tf_op jit(solution)/shard_map/ppermute | solution.py:173
  24.4 2.3 %collective-permute-start.8 = (bf16[4,7168]{1,0:T(4,128)(2,1)S(1)}, bf16[4,7168]{1,0:T(4,128)(2,1)S(1)}, u32[]{:S(2)}, u32[]{:S(2)}) collective-permute-start(bf16[4,7168]{1,0:T(4,128)(2,1)S(1)} %get-tuple-element.16), channel_id=1, source_target_pairs={{0,6},{2,4},{4,2},{6,0},{8,14},{10,12},{12,10},{14,8},{1,7},{3,5},... | collective-permute-start | bytes 172040 | tf_op jit(solution)/shard_map/ppermute | solution.py:173
  26.7 0.7 %collective-permute-done.6 = bf16[4,7168]{1,0:T(4,128)(2,1)S(1)} collective-permute-done((bf16[4,7168]{1,0:T(4,128)(2,1)S(1)}, bf16[4,7168]{1,0:T(4,128)(2,1)S(1)}, u32[]{:S(2)}, u32[]{:S(2)}) %collective-permute-start.6) | collective-permute-done | bytes 57376 | tf_op jit(solution)/shard_map/ppermute | solution.py:173
  27.4 0.9 %collective-permute-done.7 = bf16[4,7168]{1,0:T(4,128)(2,1)S(1)} collective-permute-done((bf16[4,7168]{1,0:T(4,128)(2,1)S(1)}, bf16[4,7168]{1,0:T(4,128)(2,1)S(1)}, u32[]{:S(2)}, u32[]{:S(2)}) %collective-permute-start.7) | collective-permute-done | bytes 57376 | tf_op jit(solution)/shard_map/ppermute | solution.py:173
  28.3 1.3 %collective-permute-done.8 = bf16[4,7168]{1,0:T(4,128)(2,1)S(1)} collective-permute-done((bf16[4,7168]{1,0:T(4,128)(2,1)S(1)}, bf16[4,7168]{1,0:T(4,128)(2,1)S(1)}, u32[]{:S(2)}, u32[]{:S(2)}) %collective-permute-start.8) | collective-permute-done | bytes 57376 | tf_op jit(solution)/shard_map/ppermute | solution.py:173
  29.7 2.8 %collective-permute-start.9 = (bf16[2,7168]{1,0:T(2,128)(2,1)S(1)}, bf16[2,7168]{1,0:T(2,128)(2,1)S(1)}, u32[]{:S(2)}, u32[]{:S(2)}) collective-permute-start(bf16[2,7168]{1,0:T(2,128)(2,1)S(1)} %slice.37), channel_id=1, source_target_pairs={{0,8},{2,10},{4,12},{6,14},{8,0},{10,2},{12,4},{14,6},{1,9},{3,11}... | collective-permute-start | bytes 86024 | tf_op jit(solution)/shard_map/ppermute | solution.py:173
  32.6 0.2 shard_map.64.weight_ref
  32.8 1.8 %collective-permute-done.9.refs_1_ = bf16[2,7168]{1,0:T(2,128)(2,1)S(1)} collective-permute-done((bf16[2,7168]{1,0:T(2,128)(2,1)S(1)}, bf16[2,7168]{1,0:T(2,128)(2,1)S(1)}, u32[]{:S(2)}, u32[]{:S(2)}) %collective-permute-start.9) | collective-permute-done | bytes 28704 | tf_op jit(solution)/shard_map/ppermute | solution.py:173
  34.5 1.6 %shard_map.70 = bf16[64,7168]{1,0:T(8,128)(2,1)} custom-call(f32[64,128]{1,0:T(8,128)S(1)} %shard_map.64.weight_ref, f32[4,7168]{1,0:T(4,128)S(1)} %fusion.2.refs_0_, bf16[2,7168]{1,0:T(2,128)(2,1)S(1)} %collective-permute-done.9.refs_1_), custom_call_target="tpu_custom_call" | custom-call | tf_op jit(solution)/shard_map/pallas_call | solution.py:153
  (17 shorter events, 0.7 us)
Async XLA Ops:
  1.5 14.8 %copy-start = (bf16[256,7168]{1,0:T(8,128)(2,1)S(1)}, bf16[256,7168]{1,0:T(8,128)(2,1)}, u32[]{:S(2)}) copy-start(bf16[256,7168]{1,0:T(8,128)(2,1)} %source_ref.1) | copy-start | bytes 11010052
  1.5 6.0 %collective-permute-start = (bf16[2,7168]{1,0:T(2,128)(2,1)S(1)}, bf16[2,7168]{1,0:T(2,128)(2,1)S(1)}, u32[]{:S(2)}, u32[]{:S(2)}) collective-permute-start(bf16[2,7168]{1,0:T(2,128)(2,1)S(1)} %get-tuple-element.10), channel_id=1, source_target_pairs={{0,8},{2,10},{4,12},{6,14},{8,0},{10,2},{12,4},{14,6},{1,9},{3,11}... | collective-permute-start | bytes 86024 | tf_op jit(solution)/shard_map/ppermute | solution.py:173
  7.5 4.4 %collective-permute-start.1 = (bf16[4,7168]{1,0:T(4,128)(2,1)S(1)}, bf16[4,7168]{1,0:T(4,128)(2,1)S(1)}, u32[]{:S(2)}, u32[]{:S(2)}) collective-permute-start(bf16[4,7168]{1,0:T(4,128)(2,1)S(1)} %shard_map.66.refs_0_), channel_id=1, source_target_pairs={{0,2},{2,0},{4,6},{6,4},{8,10},{10,8},{12,14},{14,12},{1,3},{3,1},... | collective-permute-start | bytes 172040 | tf_op jit(solution)/shard_map/ppermute | solution.py:173
  9.6 4.2 %collective-permute-start.2 = (bf16[4,7168]{1,0:T(4,128)(2,1)S(1)}, bf16[4,7168]{1,0:T(4,128)(2,1)S(1)}, u32[]{:S(2)}, u32[]{:S(2)}) collective-permute-start(bf16[4,7168]{1,0:T(4,128)(2,1)S(1)} %shard_map.66.refs_0_), channel_id=1, source_target_pairs={{0,4},{2,6},{4,0},{6,2},{8,12},{10,14},{12,8},{14,10},{1,5},{3,7},... | collective-permute-start | bytes 172040 | tf_op jit(solution)/shard_map/ppermute | solution.py:173
  11.0 5.1 %collective-permute-start.3 = (bf16[4,7168]{1,0:T(4,128)(2,1)S(1)}, bf16[4,7168]{1,0:T(4,128)(2,1)S(1)}, u32[]{:S(2)}, u32[]{:S(2)}) collective-permute-start(bf16[4,7168]{1,0:T(4,128)(2,1)S(1)} %shard_map.66.refs_0_), channel_id=1, source_target_pairs={{0,6},{2,4},{4,2},{6,0},{8,14},{10,12},{12,10},{14,8},{1,7},{3,5},... | collective-permute-start | bytes 172040 | tf_op jit(solution)/shard_map/ppermute | solution.py:173
  16.1 2.0 %copy-start.1 = (bf16[7168,256]{1,0:T(8,128)(2,1)S(1)}, bf16[7168,256]{1,0:T(8,128)(2,1)}, u32[]{:S(2)}) copy-start(bf16[7168,256]{1,0:T(8,128)(2,1)} %gate_ref.1) | copy-start | bytes 11010052
  16.1 3.2 %copy-start.2 = (bf16[7168,256]{1,0:T(8,128)(2,1)S(1)}, bf16[7168,256]{1,0:T(8,128)(2,1)}, u32[]{:S(2)}) copy-start(bf16[7168,256]{1,0:T(8,128)(2,1)} %up_ref.1) | copy-start | bytes 11010052
  16.2 1.6 %collective-permute-start.4 = (bf16[16,7168]{1,0:T(8,128)(2,1)S(1)}, bf16[16,7168]{1,0:T(8,128)(2,1)S(1)}, u32[]{:S(2)}, u32[]{:S(2)}) collective-permute-start(bf16[16,7168]{1,0:T(8,128)(2,1)S(1)} %shard_map.67.mine_ref), channel_id=1, source_target_pairs={{0,1},{1,0},{2,3},{3,2},{4,5},{5,4},{6,7},{7,6},{8,9},{9,8},{10,11... | collective-permute-start | bytes 688136 | tf_op jit(solution)/shard_map/ppermute | solution.py:204
  16.5 16.0 %copy-start.3 = (s32[64,8]{0,1:T(8,128)S(1)}, s32[64,8]{0,1:T(8,128)}, u32[]{:S(2)}) copy-start(s32[64,8]{0,1:T(8,128)} %param.8) | copy-start | bytes 6148
  16.5 16.0 %copy-start.4 = (f32[64,8]{0,1:T(8,128)S(1)}, f32[64,8]{0,1:T(8,128)}, u32[]{:S(2)}) copy-start(f32[64,8]{0,1:T(8,128)} %param.7) | copy-start | bytes 6148
  21.4 1.5 %collective-permute-start.5 = (bf16[4,4,7168]{2,1,0:T(4,128)(2,1)S(1)}, bf16[4,4,7168]{2,1,0:T(4,128)(2,1)S(1)}, u32[]{:S(2)}, u32[]{:S(2)}) collective-permute-start(bf16[4,4,7168]{2,1,0:T(4,128)(2,1)S(1)} %get-tuple-element.12), channel_id=1, source_target_pairs={{0,1},{1,0},{2,3},{3,2},{4,5},{5,4},{6,7},{7,6},{8,9},{9,8},{10,11... | collective-permute-start | bytes 688136 | tf_op jit(solution)/shard_map/ppermute | solution.py:206
  23.2 4.2 %collective-permute-start.6 = (bf16[4,7168]{1,0:T(4,128)(2,1)S(1)}, bf16[4,7168]{1,0:T(4,128)(2,1)S(1)}, u32[]{:S(2)}, u32[]{:S(2)}) collective-permute-start(bf16[4,7168]{1,0:T(4,128)(2,1)S(1)} %get-tuple-element.15), channel_id=1, source_target_pairs={{0,2},{2,0},{4,6},{6,4},{8,10},{10,8},{12,14},{14,12},{1,3},{3,1},... | collective-permute-start | bytes 172040 | tf_op jit(solution)/shard_map/ppermute | solution.py:173
  23.7 4.6 %collective-permute-start.7 = (bf16[4,7168]{1,0:T(4,128)(2,1)S(1)}, bf16[4,7168]{1,0:T(4,128)(2,1)S(1)}, u32[]{:S(2)}, u32[]{:S(2)}) collective-permute-start(bf16[4,7168]{1,0:T(4,128)(2,1)S(1)} %get-tuple-element.17), channel_id=1, source_target_pairs={{0,4},{2,6},{4,0},{6,2},{8,12},{10,14},{12,8},{14,10},{1,5},{3,7},... | collective-permute-start | bytes 172040 | tf_op jit(solution)/shard_map/ppermute | solution.py:173
  24.4 5.2 %collective-permute-start.8 = (bf16[4,7168]{1,0:T(4,128)(2,1)S(1)}, bf16[4,7168]{1,0:T(4,128)(2,1)S(1)}, u32[]{:S(2)}, u32[]{:S(2)}) collective-permute-start(bf16[4,7168]{1,0:T(4,128)(2,1)S(1)} %get-tuple-element.16), channel_id=1, source_target_pairs={{0,6},{2,4},{4,2},{6,0},{8,14},{10,12},{12,10},{14,8},{1,7},{3,5},... | collective-permute-start | bytes 172040 | tf_op jit(solution)/shard_map/ppermute | solution.py:173
  29.7 4.8 %collective-permute-start.9 = (bf16[2,7168]{1,0:T(2,128)(2,1)S(1)}, bf16[2,7168]{1,0:T(2,128)(2,1)S(1)}, u32[]{:S(2)}, u32[]{:S(2)}) collective-permute-start(bf16[2,7168]{1,0:T(2,128)(2,1)S(1)} %slice.37), channel_id=1, source_target_pairs={{0,8},{2,10},{4,12},{6,14},{8,0},{10,2},{12,4},{14,6},{1,9},{3,11}... | collective-permute-start | bytes 86024 | tf_op jit(solution)/shard_map/ppermute | solution.py:173
